TPU v7x, 32 devices: a whole 2x2x4 slice. The times are simulated.
32 devices in a mesh: mode: 8 (over z, y), cores: 4 (over x, core).
Axes of the slice: x: 2, y: 2, z: 4, core: 2. Of those that a mesh axis runs over, the one named last changes fastest.
Arguments:
- train_cores: bfloat16 [4, 400, 32, 400], P('cores', None, 'mode'), may hold values from -0.24748737 to 0.24748737
- sketch_cores: bfloat16 [4, 100, 32, 100], P('cores', None, 'mode'), may hold values from -0.3125 to 0.3125
- left_interface: float32 [100, 400], replicated, may hold values from -6 to 6
- right_sketch: bfloat16 [400, 100], replicated, may hold values from -6 to 6
Outputs:
- frames: bfloat16 [4, 100, 32, 100], P('cores', None, 'mode')
- interfaces: float32 [4, 100, 400], P('cores')
All inputs are finite; a program needn't handle non-finite values.
Results may differ from a plain program's by a relative error of at most 0.019.
Values may be sent and summed in bfloat16 or wider, within the bound.
A program may use at most 64 MiB of HBM per device.

v0:
```python
import functools
import math

import jax
import jax.numpy as jnp
from jax import lax
from jax.experimental import pallas as pl
from jax.experimental.pallas import tpu as pltpu
from jax.sharding import PartitionSpec as P

MESH = pl.DeviceIdType.MESH
F32, BF16 = jnp.float32, jnp.bfloat16
EXACT = lax.Precision.HIGHEST


def up(value, step):
    return -(-value // step) * step


def dot(a, b, ca, cb, precision=None):
    return lax.dot_general(
        a, b, (((ca,), (cb,)), ((), ())), preferred_element_type=F32, precision=precision
    )


def when(condition, run):
    if condition is True:
        run()
    else:
        pl.when(condition)(run)


def lower_inverse(gram, size, look=4):
    full = gram.shape[0]
    lane = lax.broadcasted_iota(jnp.int32, (1, full), 1)
    top, table, done = 0, gram, []
    for first in range(0, size, look):
        base = first // 8 * 8
        if base > top:
            done.append(table[: base - top])
            table = table[base - top :]
            top = base
        rows = full - top
        width = min(look, size - first)
        row_id = lax.broadcasted_iota(jnp.int32, (rows, full), 0) + top
        columns = [
            jnp.broadcast_to(table[:, first + t : first + t + 1], (rows, full)) for t in range(width)
        ]
        for t in range(width):
            j = first + t
            here = j - top
            column = columns[t]
            pivot = column[here : here + 1]
            inverse = 1.0 / pivot
            row = jnp.where(lane == j, 1.0, table[here : here + 1]) * inverse
            below = row_id > j
            lower = jnp.where(below, column, 0.0)
            for s in range(t + 1, width):
                ahead = here + s - t
                columns[s] = columns[s] - lower * (column[ahead : ahead + 1] * inverse)
            table = jnp.where((lane == j) & below, 0.0, table) - lower * row
    done.append(table)
    table = jnp.concatenate(done, axis=0) if len(done) > 1 else table
    row_id = lax.broadcasted_iota(jnp.int32, (full, full), 0)
    lane = lax.broadcasted_iota(jnp.int32, (full, full), 1)
    pivots = jnp.sum(jnp.where(row_id == lane, table, 0.0), axis=1, keepdims=True)
    unit = jnp.where(row_id > lane, table, jnp.where(row_id == lane, 1.0, 0.0))
    return unit * lax.rsqrt(pivots)


def kernel(
    dims,
    core_ref,
    gauss_ref,
    left_ref,
    right_ref,
    frames_ref,
    faces_ref,
    sketch_buf,
    part_out,
    part_in,
    carry_buf,
    carry_own,
    proj_out,
    proj_in,
    gram_out,
    gram_in,
    piece_sk,
    piece_ca,
    s_part,
    r_part,
    s_sk,
    r_sk,
    s_proj,
    r_proj,
    s_gram,
    r_gram,
    s_next,
    r_next,
    s_own,
    r_own,
):
    size, group_count, rank, sketch, modes, chunk, owners, scale = dims
    rank_pad, sketch_pad = sketch_buf.shape
    me = lax.axis_index("mode")
    group = lax.axis_index("cores")
    final = group_count - 1
    owner = True if owners == size else me < owners
    down = lax.rem(group + group_count - 1, group_count)
    upward = lax.rem(group + 1, group_count)

    barrier = pltpu.get_barrier_semaphore()

    def greet(to_group, first):
        for d in range(first, size):
            pl.semaphore_signal(
                barrier,
                inc=1,
                device_id={"mode": lax.rem(me + d, size), "cores": to_group},
                device_id_type=MESH,
            )

    greet(group, 1)
    pl.when(group < final)(lambda: greet(upward, 0))
    pl.when(group > 0)(lambda: greet(down, 0))

    @pl.when(group == 0)
    def _():
        pl.semaphore_wait(barrier, 2 * size - 1)

    @pl.when((group > 0) & (group < final))
    def _():
        pl.semaphore_wait(barrier, 3 * size - 1)

    def block(ref, index):
        return ref.at[pl.ds(pl.multiple_of(index * chunk, chunk), chunk)]

    def scatter(out_ref, in_ref, sends, recvs, whole=False):
        copies = []
        for d in range(1, size):
            peer = lax.rem(me + d, size)
            copies.append(
                pltpu.make_async_remote_copy(
                    src_ref=out_ref if whole else block(out_ref, peer),
                    dst_ref=in_ref.at[d],
                    send_sem=sends.at[d],
                    recv_sem=recvs.at[d],
                    device_id={"mode": peer},
                    device_id_type=MESH,
                )
            )
        return copies

    def chunk_sends(copies, act):
        for d, copy in enumerate(copies, 1):
            peer = lax.rem(me + d, size)
            when(True if owners == size else peer < owners, functools.partial(act, copy))

    def spread(piece_ref, buf_ref, sends, recvs, to_group, first):
        copies = []
        for d in range(first, size):
            peer = lax.rem(me + d, size)
            copies.append(
                pltpu.make_async_remote_copy(
                    src_ref=piece_ref,
                    dst_ref=block(buf_ref, me),
                    send_sem=sends.at[d],
                    recv_sem=recvs.at[me],
                    device_id={"mode": peer, "cores": to_group},
                    device_id_type=MESH,
                )
            )
        return copies

    def await_chunk(buf_ref, recvs, source):
        pltpu.make_async_remote_copy(
            src_ref=block(buf_ref, source),
            dst_ref=block(buf_ref, source),
            send_sem=recvs.at[source],
            recv_sem=recvs.at[source],
            device_id={"mode": lax.rem(me + 1, size)},
            device_id_type=MESH,
        ).wait_recv()

    if rank_pad > rank:
        proj_out[pl.ds(rank, rank_pad - rank), :] = jnp.zeros((rank_pad - rank, sketch_pad), F32)
    part_out[...] = jnp.zeros(part_out.shape, part_out.dtype)

    @pl.when(group == final)
    def _():
        sketch_buf[...] = jnp.zeros(sketch_buf.shape, BF16)
        sketch_buf[pl.ds(0, rank), pl.ds(0, sketch)] = right_ref[...]

    @pl.when(group < final)
    def _():
        for source in range(owners):
            await_chunk(sketch_buf, r_sk, source)

    part_copies = scatter(part_out, part_in, s_part, r_part)
    sk_copies = spread(piece_sk, sketch_buf, s_sk, r_sk, down, 0)
    held = sketch_buf[pl.ds(0, rank), :]
    partials = [dot(core_ref[i], held, 1, 0).astype(BF16) for i in range(modes)]

    @pl.when(group > 0)
    def _():
        total = None
        for i in range(modes):
            term = dot(partials[i][:, :sketch], gauss_ref[i], 1, 1)
            total = term if total is None else total + term
        part_out[pl.ds(0, rank), pl.ds(0, sketch)] = total.astype(part_out.dtype)

        @pl.when(group == final)
        def _():
            pl.semaphore_wait(barrier, 2 * size - 1)

        chunk_sends(part_copies, lambda c: c.start())

        def finish():
            value = block(part_out, me)[...].astype(F32)
            for d in range(1, size):
                part_copies[d - 1].wait_recv()
                value = value + part_in[d].astype(F32)
            piece_sk[...] = value.astype(BF16)
            for copy in sk_copies:
                copy.start()
            for copy in sk_copies:
                copy.wait_send()

        when(owner, finish)
        chunk_sends(part_copies, lambda c: c.wait_send())

    @pl.when(group == 0)
    def _():
        carry_buf[...] = jnp.zeros(carry_buf.shape, BF16)
        carry_buf[pl.ds(0, rank), pl.ds(0, sketch)] = left_ref[...].T.astype(BF16)

    @pl.when(group > 0)
    def _():
        for source in range(owners):
            await_chunk(carry_buf, r_next, source)

    carry = carry_buf[pl.ds(0, rank), :].T
    gram_copies = scatter(gram_out, gram_in, s_gram, r_gram, True)
    proj_copies = scatter(proj_out, proj_in, s_proj, r_proj)
    images = [dot(carry, partials[i], 1, 0) for i in range(modes)]
    image = jnp.concatenate(images, axis=0)
    high = image.astype(BF16)
    low = (image - high.astype(F32)).astype(BF16)
    pair = jnp.concatenate([high, low], axis=1)
    terms = dot(high, pair, 0, 0)
    cross = terms[:, sketch_pad:]
    gram = terms[:, :sketch_pad] + cross + cross.T
    half, quarter = sketch_pad // 2, sketch_pad // 4
    lower_rows = gram_out.shape[0] - quarter
    gram_out[pl.ds(0, lower_rows), :] = gram[half : half + lower_rows]
    gram_out[pl.ds(lower_rows, quarter), :] = jnp.concatenate(
        [gram[:quarter, :half], gram[quarter:half, :half]], axis=1
    )
    for copy in gram_copies:
        copy.start()
    built = jnp.concatenate(
        [dot(carry, core_ref[i], 1, 0).astype(BF16) for i in range(modes)], axis=0
    )
    proj = dot(built, pair, 0, 0)
    proj_out[pl.ds(0, rank), :] = proj[:, :sketch_pad] + proj[:, sketch_pad:]
    chunk_sends(proj_copies, lambda c: c.start())

    gram_in[0] = gram_out[...]
    for copy in gram_copies:
        copy.wait_recv()
    total = None
    for source in range(size):
        term = gram_in[lax.rem(me - source + size, size)]
        total = term if total is None else total + term
    lower = total[:lower_rows]
    if lower_rows < half:
        lower = jnp.concatenate([lower, jnp.zeros((half - lower_rows, sketch_pad), F32)], axis=0)
    corner = total[lower_rows:]
    corner = jnp.concatenate([corner[:, :half], corner[:, half:]], axis=0)
    upper = jnp.concatenate([corner, lower.T[:half]], axis=1)
    total = jnp.concatenate([upper, lower], axis=0)
    row_id = lax.broadcasted_iota(jnp.int32, (sketch_pad, sketch_pad), 0)
    lane_id = lax.broadcasted_iota(jnp.int32, (sketch_pad, sketch_pad), 1)
    total = jnp.where((row_id == lane_id) & (row_id >= sketch), 1.0, total)
    inverse = lower_inverse(total, sketch, 8)

    next_copies = spread(piece_ca, carry_buf, s_next, r_next, upward, 0)
    own_copies = spread(piece_ca, carry_own, s_own, r_own, group, 1)

    def project():
        value = block(proj_out, me)[...]
        for d in range(1, size):
            proj_copies[d - 1].wait_recv()
            value = value + proj_in[d]
        piece_ca[...] = dot(value, inverse, 1, 1, EXACT).astype(BF16)

        @pl.when(group < final)
        def _():
            for copy in next_copies:
                copy.start()

        for copy in own_copies:
            copy.start()
        block(carry_own, me)[...] = piece_ca[...]

    when(owner, project)
    orth = (dot(image, inverse, 1, 1, EXACT) * scale).astype(BF16)
    for i in range(modes):
        frames_ref[i] = orth[i * sketch_pad : (i + 1) * sketch_pad]
    chunk_sends(proj_copies, lambda c: c.wait_send())
    for copy in gram_copies:
        copy.wait_send()
    for source in range(owners):

        @pl.when(me != source)
        def _(source=source):
            await_chunk(carry_own, r_own, source)

    faces_ref[...] = carry_own[...].T.astype(F32)

    def drain():
        for copy in own_copies:
            copy.wait_send()

        @pl.when(group < final)
        def _():
            for copy in next_copies:
                copy.wait_send()

    when(owner, drain)


def body(train_cores, sketch_cores, left_interface, right_sketch):
    size = lax.axis_size("mode")
    group_count = lax.axis_size("cores")
    _, rank, modes, _ = train_cores.shape
    sketch = sketch_cores.shape[1]
    sketch_pad = up(sketch, 128)
    chunk = up(-(-up(rank, 128) // size), 16)
    owners = -(-rank // chunk)
    rank_pad = owners * chunk
    core = train_cores[0].transpose(1, 0, 2)
    gauss = sketch_cores[0].transpose(1, 0, 2)
    scale = math.sqrt(sketch * modes * size)
    dims = (size, group_count, rank, sketch, modes, chunk, owners, scale)
    gram_rows = up(max(sketch - sketch_pad // 2, 8), 8) + sketch_pad // 4
    chunks = (rank_pad, sketch_pad)
    vmem = pl.BlockSpec(memory_space=pltpu.VMEM)
    dma = pltpu.SemaphoreType.DMA((size,))
    frames, faces = pl.pallas_call(
        functools.partial(kernel, dims),
        out_shape=(
            jax.ShapeDtypeStruct((modes, sketch_pad, sketch_pad), BF16),
            jax.ShapeDtypeStruct((sketch_pad, rank_pad), F32),
        ),
        in_specs=[vmem] * 4,
        out_specs=(vmem, vmem),
        scratch_shapes=[
            pltpu.VMEM(chunks, BF16),
            pltpu.VMEM((size * chunk, sketch_pad), BF16),
            pltpu.VMEM((size, chunk, sketch_pad), BF16),
            pltpu.VMEM(chunks, BF16),
            pltpu.VMEM(chunks, BF16),
            pltpu.VMEM((size * chunk, sketch_pad), F32),
            pltpu.VMEM((size, chunk, sketch_pad), F32),
            pltpu.VMEM((gram_rows, sketch_pad), F32),
            pltpu.VMEM((size, gram_rows, sketch_pad), F32),
            pltpu.VMEM((chunk, sketch_pad), BF16),
            pltpu.VMEM((chunk, sketch_pad), BF16),
        ]
        + [dma] * 12,
        compiler_params=pltpu.CompilerParams(collective_id=0, has_side_effects=True),
    )(core, gauss, left_interface, right_sketch)
    frames = frames[:, :sketch, :sketch].transpose(1, 0, 2)[None]
    return frames, faces[None, :sketch, :rank]


def solution(mesh):
    in_specs = (P("cores", None, "mode", None), P("cores", None, "mode", None), P(), P())
    out_specs = (P("cores", None, "mode", None), P("cores", None, None))
    return jax.shard_map(body, mesh=mesh, in_specs=in_specs, out_specs=out_specs, check_vma=False)
```

profile of v0, /device:TPU:3, one launch (start us, length us, event | category | flops | bytes accessed | tf_op | source)
XLA Modules:
  0.0 99.3 jit_solution(15290957008818411397)
XLA Ops:
  0.6 1.6 %copy.14 = bf16[1,100,4,100]{3,1,2,0:T(8,128)(2,1)} copy(bf16[1,100,4,100]{3,2,1,0:T(4,128)(2,1)} %param.5) | data formatting | bytes 160000 | tf_op args[1]
  2.2 1.8 %copy.8.left_ref = f32[100,400]{1,0:T(8,128)} copy(f32[100,400]{0,1:T(8,128)} %param.6) | data formatting | bytes 320000 | tf_op args[2]
  3.9 2.9 %copy.13 = bf16[1,400,4,400]{3,1,2,0:T(8,128)(2,1)} copy(bf16[1,400,4,400]{3,2,1,0:T(4,128)(2,1)} %param.4) | data formatting | bytes 2560000 | tf_op args[0]
  6.9 88.9 %shard_map.59 = (bf16[4,128,128]{2,1,0:T(8,128)(2,1)}, f32[128,448]{1,0:T(8,128)}) custom-call(bf16[4,400,400]{2,1,0:T(8,128)(2,1)} %bitcast.16, bf16[4,100,100]{2,1,0:T(8,128)(2,1)} %bitcast.17, f32[100,400]{1,0:T(8,128)} %copy.8.left_ref, bf16[400,100]{1,0:T(8,128)(2,1)} %right_ref.1), custom_call_target="tpu_custom_call" | custom-call | tf_op jit(solution)/shard_map/pallas_call | solution.py:350
  95.8 0.9 slice_bitcast_fusion.1
  96.7 0.7 copy.9
  97.4 0.9 slice_bitcast_fusion
  98.4 0.9 copy.10
where the time goes:
time: 99.7 us; the launch traced here: 99.3 us
  Pallas kernels  88.9 us (89%)
  local copies, waits for them, and re-layouts  9.67 us (10%)
    pallas_call x1, Pallas kernels, body(): pl.pallas_call(functools.partial(kernel, dims), out_shape=(jax.ShapeDtype...  88.9 us
    unnamed x5, local copies, waits for them, and re-layouts  7.81 us

commit v1 on v0

v1 whole, which is shorter than its diff:
```python
import functools
import math

import jax
import jax.numpy as jnp
from jax import lax
from jax.experimental import pallas as pl
from jax.experimental.pallas import tpu as pltpu
from jax.sharding import PartitionSpec as P

MESH = pl.DeviceIdType.MESH
F32, BF16 = jnp.float32, jnp.bfloat16
EXACT = lax.Precision.HIGHEST
LANES = 128


def up(value, step):
    return -(-value // step) * step


def dot(a, b, ca, cb, precision=None):
    return lax.dot_general(
        a, b, (((ca,), (cb,)), ((), ())), preferred_element_type=F32, precision=precision
    )


def partner(me, d, size):
    if size & (size - 1):
        return lax.rem(me + d, size)
    other, bit = 0, 1
    while bit < size:
        digit = lax.rem(lax.div(me, bit), 2)
        other = other + bit * ((1 - digit) if d & bit else digit)
        bit *= 2
    return other


def far_first(size):
    return list(range(size - 1, 0, -1))


def owner_first(size):
    order = far_first(size)
    half = size // 2
    middle = [d for d in order if d >= half and d < half + half // 2]
    return middle + [d for d in order if d not in middle]


def lower_inverse(gram, size, look=4):
    full = gram.shape[0]
    lane = lax.broadcasted_iota(jnp.int32, (1, full), 1)
    top, table, done = 0, gram, []
    for first in range(0, size, look):
        base = first // 8 * 8
        if base > top:
            done.append(table[: base - top])
            table = table[base - top :]
            top = base
        rows = full - top
        width = min(look, size - first)
        row_id = lax.broadcasted_iota(jnp.int32, (rows, full), 0) + top
        columns = [
            jnp.broadcast_to(table[:, first + t : first + t + 1], (rows, full)) for t in range(width)
        ]
        for t in range(width):
            j = first + t
            here = j - top
            column = columns[t]
            pivot = column[here : here + 1]
            inverse = 1.0 / pivot
            row = jnp.where(lane == j, 1.0, table[here : here + 1]) * inverse
            below = row_id > j
            lower = jnp.where(below, column, 0.0)
            for s in range(t + 1, width):
                ahead = here + s - t
                columns[s] = columns[s] - lower * (column[ahead : ahead + 1] * inverse)
            table = jnp.where((lane == j) & below, 0.0, table) - lower * row
    done.append(table)
    table = jnp.concatenate(done, axis=0) if len(done) > 1 else table
    row_id = lax.broadcasted_iota(jnp.int32, (full, full), 0)
    lane = lax.broadcasted_iota(jnp.int32, (full, full), 1)
    pivots = jnp.sum(jnp.where(row_id == lane, table, 0.0), axis=1, keepdims=True)
    unit = jnp.where(row_id > lane, table, jnp.where(row_id == lane, 1.0, 0.0))
    return unit * lax.rsqrt(pivots)


def kernel(
    dims,
    core_hbm,
    gauss_hbm,
    left_hbm,
    right_hbm,
    frames_ref,
    faces_ref,
    core_ref,
    gauss_ref,
    left_ref,
    right_ref,
    slices,
    gauss,
    rows_buf,
    sketch_buf,
    part_out,
    part_in,
    carry_buf,
    carry_own,
    proj_out,
    proj_in,
    gram_out,
    gram_in,
    piece_sk,
    piece_ca,
    s_load,
    s_part,
    r_part,
    s_sk,
    r_sk,
    s_proj,
    r_proj,
    s_gram,
    r_gram,
    s_next,
    r_next,
    s_own,
    r_own,
):
    size, group_count, rank, sketch, modes, owners, scale = dims
    wide = sketch_buf.shape[1]
    tall = carry_buf.shape[1]
    me = lax.axis_index("mode")
    group = lax.axis_index("cores")
    final = group_count - 1
    first = (size - owners) // 2
    down = lax.rem(group + group_count - 1, group_count)
    upward = lax.rem(group + 1, group_count)
    extents = [min(LANES, up(rank - LANES * c, 16)) for c in range(owners)]
    last = first + owners - 1
    owner = (me >= first) & (me <= last)
    mine = jnp.clip(me - first, 0, owners - 1)

    barrier = pltpu.get_barrier_semaphore()

    def greet(peer, to_group):
        pl.semaphore_signal(
            barrier, inc=1, device_id={"mode": peer, "cores": to_group}, device_id_type=MESH
        )

    for d in far_first(size):
        greet(partner(me, d, size), group)
    for c in range(owners):
        pl.when(group < final)(lambda c=c: greet(first + c, upward))
        pl.when(group > 0)(lambda c=c: greet(first + c, down))

    loads = [
        pltpu.make_async_copy(src, dst, s_load.at[n])
        for n, (src, dst) in enumerate(
            [(right_hbm, right_ref), (core_hbm, core_ref), (gauss_hbm, gauss_ref), (left_hbm, left_ref)]
        )
    ]
    for load in loads:
        load.start()

    def meet():
        sides = (group > 0).astype(jnp.int32) + (group < final).astype(jnp.int32)
        pl.semaphore_wait(barrier, size - 1 + size * sides * owner.astype(jnp.int32))

    def scatter(out_ref, in_ref, sends, recvs):
        return [
            pltpu.make_async_remote_copy(
                src_ref=out_ref.at[pl.ds(c * LANES, extents[c])],
                dst_ref=in_ref.at[me, pl.ds(0, extents[c])],
                send_sem=sends.at[c],
                recv_sem=recvs.at[me],
                device_id={"mode": first + c},
                device_id_type=MESH,
            )
            for c in range(owners)
        ]

    def scatter_start(copies):
        def go(order):
            for c in order:
                pl.when(me != first + c)(lambda c=c: copies[c].start())

        pl.when(me < size // 2)(lambda: go(range(owners - 1, -1, -1)))
        pl.when(me >= size // 2)(lambda: go(range(owners)))

    def scatter_sent(copies):
        for c in range(owners):
            pl.when(me != first + c)(lambda c=c: copies[c].wait_send())

    def gathered(out_ref, in_ref, recvs, extent):
        value = out_ref[pl.ds(pl.multiple_of(mine * LANES, LANES), extent)].astype(F32)
        for d in far_first(size)[::-1]:
            peer = partner(me, d, size)
            landing = in_ref.at[peer, pl.ds(0, extent)]
            pltpu.make_async_remote_copy(
                src_ref=landing,
                dst_ref=landing,
                send_sem=recvs.at[peer],
                recv_sem=recvs.at[peer],
                device_id={"mode": partner(me, 1, size)},
                device_id_type=MESH,
            ).wait_recv()
            value = value + landing[...].astype(F32)
        return value

    def spread(src_ref, dst_ref, sends, recvs, to_group, home):
        return [
            pltpu.make_async_remote_copy(
                src_ref=src_ref,
                dst_ref=dst_ref,
                send_sem=sends.at[d],
                recv_sem=recvs.at[mine],
                device_id={"mode": partner(me, d, size), "cores": to_group},
                device_id_type=MESH,
            )
            for d in owner_first(size) + ([0] if home else [])
        ]

    def await_piece(dst_ref, recvs, c):
        pltpu.make_async_remote_copy(
            src_ref=dst_ref,
            dst_ref=dst_ref,
            send_sem=recvs.at[c],
            recv_sem=recvs.at[c],
            device_id={"mode": partner(me, 1, size)},
            device_id_type=MESH,
        ).wait_recv()

    def owned(run):
        if extents[-1] == LANES:
            pl.when(owner)(lambda: run(LANES))
        else:
            pl.when(owner & (me < last))(lambda: run(LANES))
            pl.when(me == last)(lambda: run(extents[-1]))

    def split():
        for i in range(modes):
            slices[i] = core_ref[:, i, :]

    part_out[...] = jnp.zeros(part_out.shape, part_out.dtype)
    if proj_out.shape[0] > rank:
        proj_out[pl.ds(rank, proj_out.shape[0] - rank), :] = jnp.zeros(
            (proj_out.shape[0] - rank, wide), F32
        )
    loads[2].wait()
    for i in range(modes):
        gauss[i] = gauss_ref[:, i, :]
    loads[0].wait()
    loads[1].wait()
    loads[3].wait()

    @pl.when(group == final)
    def _():
        sketch_buf[...] = jnp.zeros(sketch_buf.shape, BF16)
        sketch_buf[pl.ds(0, rank), pl.ds(0, sketch)] = right_ref[...]

    @pl.when(group < final)
    def _():
        split()
        meet()
        for c in range(owners):
            await_piece(sketch_buf.at[pl.ds(c * LANES, extents[c])], r_sk, c)

    part_copies = scatter(part_out, part_in, s_part, r_part)
    held = sketch_buf[pl.ds(0, rank), :]
    rows_buf[...] = dot(core_ref[...].reshape(rank * modes, rank), held, 1, 0)
    partials = [rows_buf[pl.ds(i, rank, stride=modes), :].astype(BF16) for i in range(modes)]

    @pl.when(group > 0)
    def _():
        total = None
        for i in range(modes):
            term = dot(partials[i][:, :sketch], gauss[i], 1, 1)
            total = term if total is None else total + term
        part_out[pl.ds(0, rank), pl.ds(0, sketch)] = total.astype(part_out.dtype)
        pl.when(group == final)(meet)
        scatter_start(part_copies)

        def finish(extent):
            piece = piece_sk.at[pl.ds(0, extent)]
            target = sketch_buf.at[pl.ds(pl.multiple_of(mine * LANES, LANES), extent)]
            copies = spread(piece, target, s_sk, r_sk, down, True)
            piece[...] = gathered(part_out, part_in, r_part, extent).astype(BF16)
            for copy in copies:
                copy.start()
            for copy in copies:
                copy.wait_send()

        owned(finish)
        scatter_sent(part_copies)

    pl.when(group == final)(split)

    @pl.when(group == 0)
    def _():
        carry_buf[...] = jnp.zeros(carry_buf.shape, BF16)
        carry = left_ref[...].T.astype(BF16)
        for c in range(owners):
            width = min(LANES, rank - c * LANES)
            carry_buf[c, pl.ds(0, sketch), pl.ds(0, width)] = carry[:, c * LANES : c * LANES + width]

    @pl.when(group > 0)
    def _():
        for c in range(owners):
            await_piece(carry_buf.at[c], r_next, c)

    carry = jnp.concatenate([carry_buf[c] for c in range(owners)], axis=1)[:, :rank]
    gram_copies = [
        pltpu.make_async_remote_copy(
            src_ref=gram_out,
            dst_ref=gram_in.at[me],
            send_sem=s_gram.at[d],
            recv_sem=r_gram.at[me],
            device_id={"mode": partner(me, d, size)},
            device_id_type=MESH,
        )
        for d in far_first(size)
    ]
    proj_copies = scatter(proj_out, proj_in, s_proj, r_proj)
    images = [dot(carry, partials[i], 1, 0) for i in range(modes)]
    image = jnp.concatenate(images, axis=0)
    high = image.astype(BF16)
    low = (image - high.astype(F32)).astype(BF16)
    pair = jnp.concatenate([high, low], axis=1)
    terms = dot(high, pair, 0, 0)
    cross = terms[:, wide:]
    gram = terms[:, :wide] + cross + cross.T
    half, quarter = wide // 2, wide // 4
    lower_rows = gram_out.shape[0] - quarter
    gram_out[pl.ds(0, lower_rows), :] = gram[half : half + lower_rows]
    gram_out[pl.ds(lower_rows, quarter), :] = jnp.concatenate(
        [gram[:quarter, :half], gram[quarter:half, :half]], axis=1
    )
    for copy in gram_copies:
        copy.start()
    built = jnp.concatenate(
        [dot(carry, slices[i], 1, 0).astype(BF16) for i in range(modes)], axis=0
    )
    proj = dot(built, pair, 0, 0)
    proj_out[pl.ds(0, rank), :] = proj[:, :wide] + proj[:, wide:]
    scatter_start(proj_copies)

    gram_in[me] = gram_out[...]
    for d in far_first(size)[::-1]:
        peer = partner(me, d, size)
        await_piece(gram_in.at[peer], r_gram, peer)
    total = None
    for source in range(size):
        term = gram_in[source]
        total = term if total is None else total + term
    lower = total[:lower_rows]
    if lower_rows < half:
        lower = jnp.concatenate([lower, jnp.zeros((half - lower_rows, wide), F32)], axis=0)
    corner = total[lower_rows:]
    corner = jnp.concatenate([corner[:, :half], corner[:, half:]], axis=0)
    upper = jnp.concatenate([corner, lower.T[:half]], axis=1)
    total = jnp.concatenate([upper, lower], axis=0)
    row_id = lax.broadcasted_iota(jnp.int32, (wide, wide), 0)
    lane_id = lax.broadcasted_iota(jnp.int32, (wide, wide), 1)
    total = jnp.where((row_id == lane_id) & (row_id >= sketch), 1.0, total)
    inverse = lower_inverse(total, sketch, 8)

    next_copies = spread(piece_ca, carry_buf.at[mine], s_next, r_next, upward, True)
    own_copies = spread(piece_ca, carry_own.at[mine], s_own, r_own, group, False)

    def project(extent):
        value = gathered(proj_out, proj_in, r_proj, extent)
        if extent < LANES:
            value = jnp.concatenate([value, jnp.zeros((LANES - extent, wide), F32)], axis=0)
        piece_ca[...] = dot(inverse, value, 1, 1, EXACT)[:tall].astype(BF16)

        @pl.when(group < final)
        def _():
            for copy in next_copies:
                copy.start()

        for copy in own_copies:
            copy.start()
        carry_own[mine] = piece_ca[...]

    owned(project)
    orth = dot(image, inverse, 1, 1, EXACT) * scale
    for i in range(modes):
        rows_buf[pl.ds(i, tall, stride=modes), :] = orth[i * tall : (i + 1) * tall]
    frames = rows_buf[pl.ds(0, sketch * modes), :].astype(BF16)
    frames_ref[...] = frames[:, :sketch].reshape(sketch, modes, sketch)
    scatter_sent(proj_copies)
    for copy in gram_copies:
        copy.wait_send()
    for c in range(owners):

        @pl.when(me != first + c)
        def _(c=c):
            await_piece(carry_own.at[c], r_own, c)

    faces = jnp.concatenate([carry_own[c] for c in range(owners)], axis=1)
    faces_ref[...] = faces[:sketch, :rank].astype(F32).reshape(sketch, 1, rank)

    def drain():
        for copy in own_copies:
            copy.wait_send()

        @pl.when(group < final)
        def _():
            for copy in next_copies:
                copy.wait_send()

    pl.when(owner)(drain)


def body(train_cores, sketch_cores, left_interface, right_sketch):
    size = lax.axis_size("mode")
    group_count = lax.axis_size("cores")
    _, rank, modes, _ = train_cores.shape
    sketch = sketch_cores.shape[1]
    wide, tall = up(sketch, LANES), up(sketch, 8)
    owners = -(-rank // LANES)
    deep = owners * LANES
    scale = math.sqrt(sketch * modes * size)
    dims = (size, group_count, rank, sketch, modes, owners, scale)
    gram_rows = up(max(sketch - wide // 2, 8), 8) + wide // 4
    anywhere = pl.BlockSpec(memory_space=pl.ANY)
    vmem = pl.BlockSpec(memory_space=pltpu.VMEM)
    dma = pltpu.SemaphoreType.DMA((size,))
    frames, faces = pl.pallas_call(
        functools.partial(kernel, dims),
        out_shape=(
            jax.ShapeDtypeStruct((sketch, modes, sketch), BF16),
            jax.ShapeDtypeStruct((sketch, 1, rank), F32),
        ),
        in_specs=[anywhere] * 4,
        out_specs=(vmem, vmem),
        scratch_shapes=[
            pltpu.VMEM((rank, modes, rank), BF16),
            pltpu.VMEM((sketch, modes, sketch), BF16),
            pltpu.VMEM((rank, sketch), F32),
            pltpu.VMEM((rank, sketch), BF16),
            pltpu.VMEM((modes, rank, rank), BF16),
            pltpu.VMEM((modes, sketch, sketch), BF16),
            pltpu.VMEM((rank * modes, wide), F32),
            pltpu.VMEM((deep, wide), BF16),
            pltpu.VMEM((deep, wide), BF16),
            pltpu.VMEM((size, LANES, wide), BF16),
            pltpu.VMEM((owners, tall, LANES), BF16),
            pltpu.VMEM((owners, tall, LANES), BF16),
            pltpu.VMEM((deep, wide), F32),
            pltpu.VMEM((size, LANES, wide), F32),
            pltpu.VMEM((gram_rows, wide), F32),
            pltpu.VMEM((size, gram_rows, wide), F32),
            pltpu.VMEM((LANES, wide), BF16),
            pltpu.VMEM((tall, LANES), BF16),
        ]
        + [dma] * 13,
        compiler_params=pltpu.CompilerParams(collective_id=0, has_side_effects=True),
    )(train_cores[0], sketch_cores[0], left_interface.T, right_sketch)
    return frames[None], faces[:, 0][None]


def solution(mesh):
    in_specs = (P("cores", None, "mode", None), P("cores", None, "mode", None), P(), P())
    out_specs = (P("cores", None, "mode", None), P("cores", None, None))
    return jax.shard_map(body, mesh=mesh, in_specs=in_specs, out_specs=out_specs, check_vma=False)
```

time: 99.7 us -> 86.5 us (0.87)
  Pallas kernels: 88.9 us -> 82.4 us
  local copies, waits for them, and re-layouts: 9.67 us -> 3.2 us
    pallas_call x1, Pallas kernels: 88.9 us -> 82.4 us  [body(): pl.pallas_call(functools.partial(kernel, dims), out_shape=(jax.ShapeDtype...]
    unnamed x5 -> x2, local copies, waits for them, and re-layouts: 7.81 us -> 3.2 us
    broadcast_in_dim x2 -> x0, local copies, waits for them, and re-layouts: 1.86 us -> none  [the longest x1 0.95 us: body(): return (frames, faces[None, :sketch, :rank])]
where the time goes in v1:
time: 86.5 us; the launch traced here: 86.3 us
  Pallas kernels  82.4 us (95%)
  local copies, waits for them, and re-layouts  3.2 us (4%)
    pallas_call x1, Pallas kernels, body(): pl.pallas_call(functools.partial(kernel, dims), out_shape=(jax.ShapeDtype...  82.4 us
    unnamed x2, local copies, waits for them, and re-layouts  3.2 us

profile of v1, /device:TPU:3, one launch (start us, length us, event | category | flops | bytes accessed | tf_op | source)
XLA Modules:
  0.0 86.3 jit_solution(11380169018753697632)
XLA Ops:
  0.6 82.4 %shard_map.59 = (bf16[100,4,100]{2,1,0:T(4,128)(2,1)}, f32[100,1,400]{2,1,0:T(1,128)}) custom-call(bf16[400,4,400]{2,1,0:T(4,128)(2,1)} %bitcast.5, bf16[100,4,100]{2,1,0:T(4,128)(2,1)} %bitcast.9, f32[400,100]{1,0:T(8,128)} %bitcast.7, bf16[400,100]{1,0:T(8,128)(2,1)} %right_hbm.1), custom_call_target="tpu_custom_call" | custom-call | tf_op jit(solution)/shard_map/pallas_call | solution.py:427
  83.1 1.6 %copy.8 = bf16[1,100,4,100]{3,2,1,0:T(4,128)(2,1)} copy(bf16[1,100,4,100]{3,2,1,0:T(4,128)(2,1)} %bitcast.8) | data formatting | bytes 160000
  84.6 1.6 %copy.9 = f32[1,100,400]{2,0,1:T(1,128)} copy(f32[1,100,400]{2,0,1:T(1,128)} %bitcast.6) | data formatting | bytes 320000

commit v2 on v1

v2 whole, which is shorter than its diff:
```python
import contextlib
import functools
import math

import jax
import jax.numpy as jnp
from jax import lax
from jax.experimental import pallas as pl
from jax.experimental.pallas import tpu as pltpu
from jax.sharding import PartitionSpec as P

MESH = pl.DeviceIdType.MESH
F32, BF16 = jnp.float32, jnp.bfloat16
EXACT = lax.Precision.HIGHEST
LANES = 128
scope = contextlib.nullcontext


def up(value, step):
    return -(-value // step) * step


def dot(a, b, ca, cb, precision=None):
    return lax.dot_general(
        a, b, (((ca,), (cb,)), ((), ())), preferred_element_type=F32, precision=precision
    )


def partner(me, d, size):
    if size & (size - 1):
        return lax.rem(me + d, size)
    other, bit = 0, 1
    while bit < size:
        digit = lax.rem(lax.div(me, bit), 2)
        other = other + bit * ((1 - digit) if d & bit else digit)
        bit *= 2
    return other


def far_first(size):
    return list(range(size - 1, 0, -1))


def owner_first(size):
    order = far_first(size)
    half = size // 2
    middle = [d for d in order if d >= half and d < half + half // 2]
    return middle + [d for d in order if d not in middle]


def lower_inverse(gram, size, look=4):
    full = gram.shape[0]
    lane = lax.broadcasted_iota(jnp.int32, (1, full), 1)
    top, table, done = 0, gram, []
    for first in range(0, size, look):
        base = first // 8 * 8
        if base > top:
            done.append(table[: base - top])
            table = table[base - top :]
            top = base
        rows = full - top
        width = min(look, size - first)
        row_id = lax.broadcasted_iota(jnp.int32, (rows, full), 0) + top
        columns = [
            jnp.broadcast_to(table[:, first + t : first + t + 1], (rows, full)) for t in range(width)
        ]
        for t in range(width):
            j = first + t
            here = j - top
            column = columns[t]
            pivot = column[here : here + 1]
            inverse = 1.0 / pivot
            row = jnp.where(lane == j, 1.0, table[here : here + 1]) * inverse
            below = row_id > j
            lower = jnp.where(below, column, 0.0)
            for s in range(t + 1, width):
                ahead = here + s - t
                columns[s] = columns[s] - lower * (column[ahead : ahead + 1] * inverse)
            table = jnp.where((lane == j) & below, 0.0, table) - lower * row
    done.append(table)
    table = jnp.concatenate(done, axis=0) if len(done) > 1 else table
    row_id = lax.broadcasted_iota(jnp.int32, (full, full), 0)
    lane = lax.broadcasted_iota(jnp.int32, (full, full), 1)
    pivots = jnp.sum(jnp.where(row_id == lane, table, 0.0), axis=1, keepdims=True)
    unit = jnp.where(row_id > lane, table, jnp.where(row_id == lane, 1.0, 0.0))
    return unit * lax.rsqrt(pivots)


def kernel(
    dims,
    core_hbm,
    gauss_hbm,
    left_hbm,
    right_hbm,
    frames_ref,
    faces_ref,
    core_ref,
    gauss_ref,
    left_ref,
    right_ref,
    slices,
    gauss,
    rows_buf,
    sketch_buf,
    head_buf,
    part_out,
    part_in,
    head_in,
    carry_buf,
    carry_own,
    proj_out,
    proj_in,
    gram_out,
    gram_in,
    piece_sk,
    piece_ca,
    piece_hd,
    inv_buf,
    inv_in,
    wide_out,
    wide_in,
    wide_piece,
    wide_all,
    full_hi,
    full_lo,
    s_load,
    s_part,
    r_part,
    r_head,
    s_sk,
    r_sk,
    s_hd,
    r_hd,
    s_proj,
    r_proj,
    s_gram,
    r_gram,
    s_next,
    r_next,
    s_own,
    r_own,
    s_wide,
    r_wide,
    s_all,
    r_all,
    s_twin,
    r_twin,
):
    size, group_count, rank, sketch, modes, owners, scale = dims
    wide = sketch_buf.shape[1]
    tall = carry_buf.shape[1]
    share = wide_piece.shape[0]
    me = lax.axis_index("mode")
    group = lax.axis_index("cores")
    final = group_count - 1
    first = (size - owners) // 2
    down = lax.rem(group + group_count - 1, group_count)
    upward = lax.rem(group + 1, group_count)
    extents = [min(LANES, up(rank - LANES * c, 16)) for c in range(owners)]
    last = first + owners - 1
    owner = (me >= first) & (me <= last)
    mine = jnp.clip(me - first, 0, owners - 1)
    everyone = [0] + far_first(size)[::-1]

    barrier = pltpu.get_barrier_semaphore()

    def greet(peer, to_group):
        pl.semaphore_signal(
            barrier, inc=1, device_id={"mode": peer, "cores": to_group}, device_id_type=MESH
        )

    @pl.when(group > 0)
    def _():
        for d in far_first(size):
            greet(partner(me, d, size), group)

    @pl.when(group > 1)
    def _():
        for c in range(owners):
            greet(first + c, down)

    @pl.when((group > 0) & (group < final) & owner)
    def _():
        for d in range(size):
            greet(partner(me, d, size), upward)

    @pl.when(group == 1)
    def _():
        for d in range(size):
            greet(partner(me, d, size), down)

    pl.when(group == 0)(lambda: greet(me, upward))

    loads = [
        pltpu.make_async_copy(src, dst, s_load.at[n])
        for n, (src, dst) in enumerate(
            [(right_hbm, right_ref), (core_hbm, core_ref), (gauss_hbm, gauss_ref), (left_hbm, left_ref)]
        )
    ]
    for load in loads:
        load.start()

    def meet():
        tops = ((group < final) & owner).astype(jnp.int32)

        @pl.when(group == 0)
        def _():
            pl.semaphore_wait(barrier, size)

        @pl.when(group == 1)
        def _():
            pl.semaphore_wait(barrier, size + size * tops)

        @pl.when(group > 1)
        def _():
            pl.semaphore_wait(barrier, size - 1 + owners + size * tops)

    def remote(src, dst, send, recv, peer, to_group):
        return pltpu.make_async_remote_copy(
            src_ref=src,
            dst_ref=dst,
            send_sem=send,
            recv_sem=recv,
            device_id={"mode": peer, "cores": to_group},
            device_id_type=MESH,
        )

    def await_piece(dst_ref, recv):
        remote(dst_ref, dst_ref, recv, recv, partner(me, 1, size), group).wait_recv()

    def scatter(out_ref, in_ref, sends, recvs, to_group):
        return [
            remote(
                out_ref.at[pl.ds(c * LANES, extents[c])],
                in_ref.at[me, pl.ds(0, extents[c])],
                sends.at[c],
                recvs.at[me],
                first + c,
                to_group,
            )
            for c in range(owners)
        ]

    def each(order, home, act):
        for c in order:
            if home:
                act(c)
            else:
                pl.when(me != first + c)(lambda c=c: act(c))

    def scatter_start(copies, home):
        start = lambda c: copies[c].start()
        pl.when(me < size // 2)(lambda: each(range(owners - 1, -1, -1), home, start))
        pl.when(me >= size // 2)(lambda: each(range(owners), home, start))

    def scatter_sent(copies, home):
        each(range(owners), home, lambda c: copies[c].wait_send())

    def gathered(in_ref, recvs, extent, own=None):
        if own is None:
            value = None
        else:
            value = own[pl.ds(pl.multiple_of(mine * LANES, LANES), extent)].astype(F32)
        for d in everyone[0 if own is None else 1 :]:
            peer = partner(me, d, size)
            landing = in_ref.at[peer, pl.ds(0, extent)]
            await_piece(landing, recvs.at[peer])
            term = landing[...].astype(F32)
            value = term if value is None else value + term
        return value

    def spread(src_ref, dst_ref, sends, recvs, to_group, home):
        return [
            remote(src_ref, dst_ref, sends.at[d], recvs.at[mine], partner(me, d, size), to_group)
            for d in owner_first(size) + ([0] if home else [])
        ]

    def block(ref, extent):
        return ref.at[pl.ds(pl.multiple_of(mine * LANES, LANES), extent)]

    def owned(run):
        if extents[-1] == LANES:
            pl.when(owner)(lambda: run(LANES))
        else:
            pl.when(owner & (me < last))(lambda: run(LANES))
            pl.when(me == last)(lambda: run(extents[-1]))

    def relay(in_ref, recvs, piece_ref, buf_ref, sends, lands, own=None):
        def finish(extent):
            piece = piece_ref.at[pl.ds(0, extent)]
            copies = spread(piece, block(buf_ref, extent), sends, lands, group, False)
            with scope("part_gather"):
                piece[...] = gathered(in_ref, recvs, extent, own).astype(BF16)
            for copy in copies:
                copy.start()
            block(buf_ref, extent)[...] = piece[...]

        owned(finish)
        for c in range(owners):

            @pl.when(me != first + c)
            def _(c=c):
                await_piece(buf_ref.at[pl.ds(c * LANES, extents[c])], lands.at[c])

    def relayed(piece_ref, buf_ref, sends, lands):
        def finish(extent):
            piece = piece_ref.at[pl.ds(0, extent)]
            for copy in spread(piece, block(buf_ref, extent), sends, lands, group, False):
                copy.wait_send()

        owned(finish)

    def split():
        with scope("split"):
            for i in range(modes):
                slices[i] = core_ref[:, i, :]

    def contract(held):
        rows_buf[...] = dot(core_ref[...].reshape(rank * modes, rank), held, 1, 0)
        return [rows_buf[pl.ds(i, rank, stride=modes), :].astype(BF16) for i in range(modes)]

    def fold(partials):
        total = None
        for i in range(modes):
            term = dot(partials[i][:, :sketch], gauss[i], 1, 1)
            total = term if total is None else total + term
        part_out[pl.ds(0, rank), pl.ds(0, sketch)] = total.astype(part_out.dtype)

    def factor(total):
        row_id = lax.broadcasted_iota(jnp.int32, (wide, wide), 0)
        lane_id = lax.broadcasted_iota(jnp.int32, (wide, wide), 1)
        total = jnp.where((row_id == lane_id) & (row_id >= sketch), 1.0, total)
        with scope("chol"):
            return lower_inverse(total, sketch, 8)

    def emit_frames(image, inverse):
        orth = dot(image, inverse, 1, 1, EXACT) * scale
        for i in range(modes):
            rows_buf[pl.ds(i, tall, stride=modes), :] = orth[i * tall : (i + 1) * tall]
        frames = rows_buf[pl.ds(0, sketch * modes), :].astype(BF16)
        frames_ref[...] = frames[:, :sketch].reshape(sketch, modes, sketch)

    def emit_faces():
        faces = jnp.concatenate([carry_own[c] for c in range(owners)], axis=1)
        faces_ref[...] = faces[:sketch, :rank].astype(F32).reshape(sketch, 1, rank)

    blocks = [(r, c) for r in range(owners) for c in range(r + 1)]
    tops, place = [], 0
    for r, c in blocks:
        tops.append(place)
        place += extents[r]

    @pl.when(group == 0)
    def _():
        loads[1].wait()
        loads[3].wait()
        carry = left_ref[...].T.astype(BF16)
        carry = jnp.concatenate([carry, jnp.zeros((tall - sketch, rank), BF16)], axis=0)
        with scope("build0"):
            built = [dot(carry, core_ref[:, i, :], 1, 0).astype(BF16) for i in range(modes)]
            for i in range(modes):
                slices[i, pl.ds(0, tall)] = built[i]
            stack = jnp.concatenate(built, axis=0)
            square = dot(stack, stack, 0, 0)
            pad = owners * LANES - rank
            square = jnp.concatenate([square, jnp.zeros((rank, pad), F32)], axis=1)
            square = jnp.concatenate([square, jnp.zeros((pad, rank + pad), F32)], axis=0)
            for (r, c), top in zip(blocks, tops):
                wide_out[pl.ds(top, extents[r]), :] = square[
                    r * LANES : r * LANES + extents[r], c * LANES : (c + 1) * LANES
                ]
            if wide_out.shape[0] > place:
                wide_out[pl.ds(place, wide_out.shape[0] - place), :] = jnp.zeros(
                    (wide_out.shape[0] - place, LANES), F32
                )
        loads[0].wait()
        loads[2].wait()
        meet()
        copies = []
        for d in far_first(size) + [0]:
            peer = partner(me, d, size)
            copies.append(
                remote(
                    wide_out.at[pl.ds(pl.multiple_of(peer * share, 8), share)],
                    wide_in.at[me],
                    s_wide.at[d],
                    r_wide.at[me],
                    peer,
                    upward,
                )
            )
        for copy in copies:
            copy.start()
        with scope("twin0"):
            await_piece(head_buf, r_twin.at[0])
        held = head_buf[pl.ds(0, rank), :]
        image = jnp.concatenate(
            [dot(slices[i, pl.ds(0, tall)], held, 1, 0) for i in range(modes)], axis=0
        )
        await_piece(inv_in, r_twin.at[1])
        emit_frames(image, inv_in[...])
        with scope("twin2"):
            await_piece(carry_own, r_twin.at[2])
        emit_faces()
        for copy in copies:
            copy.wait_send()

    @pl.when(group > 0)
    def _():
        part_out[...] = jnp.zeros(part_out.shape, part_out.dtype)
        if proj_out.shape[0] > rank:
            proj_out[pl.ds(rank, proj_out.shape[0] - rank), :] = jnp.zeros(
                (proj_out.shape[0] - rank, wide), F32
            )
        loads[2].wait()
        for i in range(modes):
            gauss[i] = gauss_ref[:, i, :]
        loads[0].wait()
        loads[1].wait()
        loads[3].wait()

        @pl.when(group == final)
        def _():
            sketch_buf[...] = jnp.zeros(sketch_buf.shape, BF16)
            sketch_buf[pl.ds(0, rank), pl.ds(0, sketch)] = right_ref[...]

        @pl.when(group < final)
        def _():
            split()
            with scope("meet"):
                meet()

        all_copies = [
            remote(
                wide_piece,
                wide_all.at[pl.ds(pl.multiple_of(me * share, 8), share)],
                s_all.at[d],
                r_all.at[me],
                partner(me, d, size),
                group,
            )
            for d in far_first(size)
        ]

        @pl.when(group == 1)
        def _():
            value = None
            for d in everyone:
                peer = partner(me, d, size)
                with scope("wide_wait"):
                    await_piece(wide_in.at[peer], r_wide.at[peer])
                term = wide_in[peer]
                value = term if value is None else value + term
            wide_piece[...] = value
            for copy in all_copies:
                copy.start()
            wide_all[pl.ds(pl.multiple_of(me * share, 8), share)] = value

        @pl.when(group < final)
        def _():
            with scope("relay_sk"):
                relay(part_in, r_part, piece_sk, sketch_buf, s_sk, r_sk)

        with scope("mark"):
            held = sketch_buf[pl.ds(0, rank), :]
        partials = contract(held)
        fold(partials)

        @pl.when(group == final)
        def _():
            with scope("meet3"):
                meet()

        @pl.when(group > 1)
        def _():
            part_copies = scatter(part_out, part_in, s_part, r_part, down)
            scatter_start(part_copies, True)
            pl.when(group == final)(split)
            pl.when(group < final)(lambda: relayed(piece_sk, sketch_buf, s_sk, r_sk))
            scatter_sent(part_copies, True)
            with scope("wait_carry"):
                for c in range(owners):
                    await_piece(carry_buf.at[c], r_next.at[c])

        @pl.when(group == 1)
        def _():
            part_copies = scatter(part_out, head_in, s_part, r_head, group)
            scatter_start(part_copies, False)
            with scope("all_wait"):
                for d in everyone[1:]:
                    peer = partner(me, d, size)
                    await_piece(
                        wide_all.at[pl.ds(pl.multiple_of(peer * share, 8), share)], r_all.at[peer]
                    )
            with scope("unpack"):
                tile = {}
                for (r, c), top in zip(blocks, tops):
                    value = wide_all[pl.ds(top, extents[r]), :]
                    if extents[r] < LANES:
                        value = jnp.concatenate(
                            [value, jnp.zeros((LANES - extents[r], LANES), F32)], axis=0
                        )
                    tile[r, c] = value
                    if r > c:
                        tile[c, r] = value.T
                for r in range(owners):
                    row = jnp.concatenate([tile[r, c] for c in range(owners)], axis=1)
                    high = row.astype(BF16)
                    full_hi[pl.ds(r * LANES, LANES)] = high
                    full_lo[pl.ds(r * LANES, LANES)] = (row - high.astype(F32)).astype(BF16)
            with scope("relay_hd"):
                relay(head_in, r_head, piece_hd, head_buf, s_hd, r_hd, part_out)
            twins = [
                remote(src, dst, s_twin.at[n], r_twin.at[n], me, down)
                for n, (src, dst) in enumerate(
                    [(head_buf, head_buf), (inv_buf, inv_in), (carry_buf, carry_own)]
                )
            ]
            twins[0].start()
            with scope("image0"):
                held = head_buf[pl.ds(0, rank), :]
                spread_y = (
                    dot(full_hi[:, :rank], held, 1, 0) + dot(full_lo[:, :rank], held, 1, 0)
                )[:rank]
                high = spread_y.astype(BF16)
                low = (spread_y - high.astype(F32)).astype(BF16)
                terms = dot(held, jnp.concatenate([high, low], axis=1), 0, 0)
            inverse = factor(terms[:, :wide] + terms[:, wide:])
            inv_buf[...] = inverse
            twins[1].start()
            carry = dot(inverse, spread_y, 1, 1, EXACT)[:tall].astype(BF16)
            for c in range(owners):
                width = min(LANES, rank - c * LANES)
                if width < LANES:
                    carry_buf[c] = jnp.zeros((tall, LANES), BF16)
                carry_buf[c, :, pl.ds(0, width)] = carry[:, c * LANES : c * LANES + width]
            twins[2].start()
            relayed(piece_sk, sketch_buf, s_sk, r_sk)
            relayed(piece_hd, head_buf, s_hd, r_hd)
            scatter_sent(part_copies, False)
            for copy in all_copies:
                copy.wait_send()
            for twin in twins:
                twin.wait_send()

        carry = jnp.concatenate([carry_buf[c] for c in range(owners)], axis=1)[:, :rank]
        partials = [rows_buf[pl.ds(i, rank, stride=modes), :].astype(BF16) for i in range(modes)]
        gram_copies = [
            remote(
                gram_out, gram_in.at[me], s_gram.at[d], r_gram.at[me], partner(me, d, size), group
            )
            for d in far_first(size)
        ]
        proj_copies = scatter(proj_out, proj_in, s_proj, r_proj, group)
        images = [dot(carry, partials[i], 1, 0) for i in range(modes)]
        image = jnp.concatenate(images, axis=0)
        high = image.astype(BF16)
        low = (image - high.astype(F32)).astype(BF16)
        pair = jnp.concatenate([high, low], axis=1)
        terms = dot(high, pair, 0, 0)
        cross = terms[:, wide:]
        gram = terms[:, :wide] + cross + cross.T
        half, quarter = wide // 2, wide // 4
        lower_rows = gram_out.shape[0] - quarter
        gram_out[pl.ds(0, lower_rows), :] = gram[half : half + lower_rows]
        gram_out[pl.ds(lower_rows, quarter), :] = jnp.concatenate(
            [gram[:quarter, :half], gram[quarter:half, :half]], axis=1
        )
        with scope("gram_send"):
            for copy in gram_copies:
                copy.start()
        built = jnp.concatenate(
            [dot(carry, slices[i], 1, 0).astype(BF16) for i in range(modes)], axis=0
        )
        proj = dot(built, pair, 0, 0)
        proj_out[pl.ds(0, rank), :] = proj[:, :wide] + proj[:, wide:]
        scatter_start(proj_copies, False)
        gram_in[me] = gram_out[...]
        with scope("gram_wait"):
            for d in everyone[1:]:
                peer = partner(me, d, size)
                await_piece(gram_in.at[peer], r_gram.at[peer])
        total = None
        for source in range(size):
            term = gram_in[source]
            total = term if total is None else total + term
        lower = total[:lower_rows]
        if lower_rows < half:
            lower = jnp.concatenate([lower, jnp.zeros((half - lower_rows, wide), F32)], axis=0)
        corner = total[lower_rows:]
        corner = jnp.concatenate([corner[:, :half], corner[:, half:]], axis=0)
        upper = jnp.concatenate([corner, lower.T[:half]], axis=1)
        inverse = factor(jnp.concatenate([upper, lower], axis=0))

        next_copies = spread(piece_ca, carry_buf.at[mine], s_next, r_next, upward, True)
        own_copies = spread(piece_ca, carry_own.at[mine], s_own, r_own, group, False)

        def project(extent):
            with scope("proj_gather"):
                value = gathered(proj_in, r_proj, extent, proj_out)
            if extent < LANES:
                value = jnp.concatenate([value, jnp.zeros((LANES - extent, wide), F32)], axis=0)
            piece_ca[...] = dot(inverse, value, 1, 1, EXACT)[:tall].astype(BF16)

            @pl.when(group < final)
            def _():
                for copy in next_copies:
                    copy.start()

            for copy in own_copies:
                copy.start()
            carry_own[mine] = piece_ca[...]

        owned(project)
        emit_frames(image, inverse)
        scatter_sent(proj_copies, False)
        for copy in gram_copies:
            copy.wait_send()
        with scope("wait_own"):
            for c in range(owners):

                @pl.when(me != first + c)
                def _(c=c):
                    await_piece(carry_own.at[c], r_own.at[c])

        emit_faces()

        def drain():
            for copy in own_copies:
                copy.wait_send()

            @pl.when(group < final)
            def _():
                for copy in next_copies:
                    copy.wait_send()

        pl.when(owner)(drain)


def body(train_cores, sketch_cores, left_interface, right_sketch):
    size = lax.axis_size("mode")
    group_count = lax.axis_size("cores")
    _, rank, modes, _ = train_cores.shape
    sketch = sketch_cores.shape[1]
    wide, tall = up(sketch, LANES), up(sketch, 8)
    owners = -(-rank // LANES)
    deep = owners * LANES
    scale = math.sqrt(sketch * modes * size)
    dims = (size, group_count, rank, sketch, modes, owners, scale)
    gram_rows = up(max(sketch - wide // 2, 8), 8) + wide // 4
    packed = LANES * owners * (owners - 1) // 2 + owners * up(rank - LANES * (owners - 1), 16)
    share = up(-(-packed // size), 8)
    anywhere = pl.BlockSpec(memory_space=pl.ANY)
    vmem = pl.BlockSpec(memory_space=pltpu.VMEM)
    dma = pltpu.SemaphoreType.DMA((size,))
    frames, faces = pl.pallas_call(
        functools.partial(kernel, dims),
        out_shape=(
            jax.ShapeDtypeStruct((sketch, modes, sketch), BF16),
            jax.ShapeDtypeStruct((sketch, 1, rank), F32),
        ),
        in_specs=[anywhere] * 4,
        out_specs=(vmem, vmem),
        scratch_shapes=[
            pltpu.VMEM((rank, modes, rank), BF16),
            pltpu.VMEM((sketch, modes, sketch), BF16),
            pltpu.VMEM((rank, sketch), F32),
            pltpu.VMEM((rank, sketch), BF16),
            pltpu.VMEM((modes, rank, rank), BF16),
            pltpu.VMEM((modes, sketch, sketch), BF16),
            pltpu.VMEM((rank * modes, wide), F32),
            pltpu.VMEM((deep, wide), BF16),
            pltpu.VMEM((deep, wide), BF16),
            pltpu.VMEM((deep, wide), BF16),
            pltpu.VMEM((size, LANES, wide), BF16),
            pltpu.VMEM((size, LANES, wide), BF16),
            pltpu.VMEM((owners, tall, LANES), BF16),
            pltpu.VMEM((owners, tall, LANES), BF16),
            pltpu.VMEM((deep, wide), F32),
            pltpu.VMEM((size, LANES, wide), F32),
            pltpu.VMEM((gram_rows, wide), F32),
            pltpu.VMEM((size, gram_rows, wide), F32),
            pltpu.VMEM((LANES, wide), BF16),
            pltpu.VMEM((tall, LANES), BF16),
            pltpu.VMEM((LANES, wide), BF16),
            pltpu.VMEM((wide, wide), F32),
            pltpu.VMEM((wide, wide), F32),
            pltpu.VMEM((size * share, LANES), F32),
            pltpu.VMEM((size, share, LANES), F32),
            pltpu.VMEM((share, LANES), F32),
            pltpu.VMEM((size * share, LANES), F32),
            pltpu.VMEM((deep, deep), BF16),
            pltpu.VMEM((deep, deep), BF16),
        ]
        + [dma] * 22,
        compiler_params=pltpu.CompilerParams(collective_id=0, has_side_effects=True),
    )(train_cores[0], sketch_cores[0], left_interface.T, right_sketch)
    return frames[None], faces[:, 0][None]


def solution(mesh):
    in_specs = (P("cores", None, "mode", None), P("cores", None, "mode", None), P(), P())
    out_specs = (P("cores", None, "mode", None), P("cores", None, None))
    return jax.shard_map(body, mesh=mesh, in_specs=in_specs, out_specs=out_specs, check_vma=False)
```

time: 86.5 us -> 81.2 us (0.939)
  Pallas kernels: 82.4 us -> 77.2 us
    pallas_call x1, Pallas kernels: 82.4 us -> 77.2 us  [body(): pl.pallas_call(functools.partial(kernel, dims), out_shape=(jax.ShapeDtype...]
where the time goes in v2:
time: 81.2 us; the launch traced here: 81 us
  Pallas kernels  77.2 us (95%)
  local copies, waits for them, and re-layouts  3.2 us (4%)
    pallas_call x1, Pallas kernels, body(): pl.pallas_call(functools.partial(kernel, dims), out_shape=(jax.ShapeDtype...  77.2 us
    unnamed x2, local copies, waits for them, and re-layouts  3.2 us

profile of v2, /device:TPU:3, one launch (start us, length us, event | category | flops | bytes accessed | tf_op | source)
XLA Modules:
  0.0 81.0 jit_solution(17139637737942383222)
XLA Ops:
  0.6 77.2 %shard_map.59 = (bf16[100,4,100]{2,1,0:T(4,128)(2,1)}, f32[100,1,400]{2,1,0:T(1,128)}) custom-call(bf16[400,4,400]{2,1,0:T(4,128)(2,1)} %bitcast.5, bf16[100,4,100]{2,1,0:T(4,128)(2,1)} %bitcast.9, f32[400,100]{1,0:T(8,128)} %bitcast.7, bf16[400,100]{1,0:T(8,128)(2,1)} %right_hbm.1), custom_call_target="tpu_custom_call" | custom-call | tf_op jit(solution)/shard_map/pallas_call | solution.py:656
  77.8 1.6 %copy.8 = bf16[1,100,4,100]{3,2,1,0:T(4,128)(2,1)} copy(bf16[1,100,4,100]{3,2,1,0:T(4,128)(2,1)} %bitcast.8) | data formatting | bytes 160000
  79.4 1.6 %copy.9 = f32[1,100,400]{2,0,1:T(1,128)} copy(f32[1,100,400]{2,0,1:T(1,128)} %bitcast.6) | data formatting | bytes 320000
